TPU v7x, 32 devices: a whole 2x2x4 slice. The times are simulated.
32 devices in a mesh: owner: 8 (over z, y), sub: 4 (over x, core).
Axes of the slice: x: 2, y: 2, z: 4, core: 2. Of those that a mesh axis runs over, the one named last changes fastest.
Arguments:
- velocity: float32 [6, 16384], P(None, 'owner'), may hold values from -6 to 6
- properties: float32 [4, 16384], P(None, 'owner'), may hold values from 0.3 to 3
- first_body: int32 [262144], P(('owner', 'sub')), may hold values from 0 to 16383, as said below
- second_body: int32 [262144], P(('owner', 'sub')), may hold values from 0 to 16383, as said below
- geometry: float32 [9, 262144], P(None, ('owner', 'sub')), may hold values from -2 to 2, as said below
- target_speed: float32 [262144], P(('owner', 'sub')), may hold values from -1 to 2
- warm_impulse: float32 [262144], P(('owner', 'sub')), may hold values from 0 to 0.5
- live_pairs: int32 [2048], P(('owner', 'sub')), may hold values from 0 to 128, as said below
Outputs:
- velocity_out: float32 [6, 16384], P(None, 'owner')
- impulse_out: float32 [262144], P(('owner', 'sub'))
Inputs may be any that keep to these rules, and one draw needn't show every extreme that they name: Pair slots are ordered by device of owner+sub, then by partner owner, then by 8 blocks of 128 slots; a slot on a device of owner o with partner owner q has first_body in [o * 2048, (o+1) * 2048) and second_body in [q * 2048, (q+1) * 2048). `second_body`: see first_body. `live_pairs`: on every device the first block toward its own owner is full; live counts differ strongly between devices and between partner owners. `geometry`: rows 0 to 2 of every column have unit length.
All inputs are finite; a program needn't handle non-finite values.
Results may differ from a plain program's by a relative error of at most 0.0001.
Values sent between devices are 32-bit elements; how exact they have to be, the bound alone decides.
A program may use at most 128 MiB of HBM per device.

v0:
```python
import functools

import jax
import jax.numpy as jnp
from jax import lax
from jax.experimental import pallas as pl
from jax.experimental.pallas import tpu as pltpu
from jax.sharding import PartitionSpec as P

ITERS = 4
LANES = 128
VEL = 6
PROPS = 4
relax = 0.1
MESH = pl.DeviceIdType.MESH


def cross_rows(left, right):
    return [
        left[1] * right[2] - left[2] * right[1],
        left[2] * right[0] - left[0] * right[2],
        left[0] * right[1] - left[1] * right[0],
    ]


def around(index, shift, size):
    return lax.rem(index + shift + size, size)


def greet(groups, subs, owner, sub):
    barrier = pltpu.get_barrier_semaphore()

    def signal(shift, carry):
        where = (around(owner, shift, groups), sub)
        pl.semaphore_signal(barrier, inc=1, device_id=where, device_id_type=MESH)
        return carry

    lax.fori_loop(1, groups, signal, 0)
    for j in range(1, subs):
        where = (owner, around(sub, j, subs))
        pl.semaphore_signal(barrier, inc=1, device_id=where, device_id_type=MESH)
    pl.semaphore_wait(barrier, groups + subs - 2)


def remote(source, target, send_sem, recv_sem, where):
    return pltpu.make_async_remote_copy(
        src_ref=source,
        dst_ref=target,
        send_sem=send_sem,
        recv_sem=recv_sem,
        device_id=where,
        device_id_type=MESH,
    )


def gather_all(groups, subs, owner, sub, piece_ref, full_ref, send3, recv3, send4, recv4):
    def across(k, slot):
        where = (around(owner, k, groups), sub)
        return remote(piece_ref, full_ref.at[slot], send3.at[k - 1], recv3.at[k - 1], where)

    def along(j, k, source, slot):
        where = (owner, around(sub, j, subs))
        return remote(source, full_ref.at[slot], send4.at[j - 1, k], recv4.at[j - 1, k], where)

    def start(k, carry):
        across(k, owner * subs + sub).start()
        return carry

    def relay(k, carry):
        slot = around(owner, -k, groups) * subs + sub
        across(k, slot).wait_recv()
        for j in range(1, subs):
            along(j, k, full_ref.at[slot], slot).start()
        return carry

    def finish(k, carry):
        for j in range(1, subs):
            slot = around(owner, -k, groups) * subs + around(sub, -j, subs)
            along(j, k, piece_ref, slot).wait()
        return carry

    def sent(k, carry):
        across(k, owner * subs + sub).wait_send()
        return carry

    lax.fori_loop(1, groups, start, 0)
    for j in range(1, subs):
        along(j, 0, piece_ref, owner * subs + sub).start()
    lax.fori_loop(1, groups, relay, 0)
    lax.fori_loop(0, groups, finish, 0)
    lax.fori_loop(1, groups, sent, 0)


def share_kernel(groups, subs, piece_ref, full_ref, send3, recv3, send4, recv4):
    owner, sub = lax.axis_index("owner"), lax.axis_index("sub")
    full_ref[owner * subs + sub] = piece_ref[...]
    greet(groups, subs, owner, sub)
    gather_all(groups, subs, owner, sub, piece_ref, full_ref, send3, recv3, send4, recv4)


def reduce_share_kernel(
    groups, subs, last, delta_ref, own_ref, full_ref, piece_ref, held1, held2, reduced,
    send1, recv1, send2, recv2, send3, recv3, send4, recv4
):
    owner, sub = lax.axis_index("owner"), lax.axis_index("sub")
    greet(groups, subs, owner, sub)

    def inner(k, j):
        q, there = around(owner, k, groups), around(sub, j, subs)
        return remote(
            delta_ref.at[q * subs + there],
            held1.at[j - 1, k],
            send1.at[j - 1, k],
            recv1.at[j - 1, k],
            (owner, there),
        )

    def outer(k):
        where = (around(owner, k, groups), sub)
        return remote(
            reduced.at[k - 1], held2.at[k - 1], send2.at[k - 1], recv2.at[k - 1], where
        )

    def start(k, carry):
        for j in range(1, subs):
            inner(k, j).start()
        return carry

    def summed(k):
        total = delta_ref[around(owner, k, groups) * subs + sub]
        for j in range(1, subs):
            inner(k, j).wait_recv()
            total += held1[j - 1, k]
        return total

    def pass_on(k, carry):
        reduced[k - 1] = summed(k)
        outer(k).start()
        return carry

    def take(k, total):
        outer(k).wait()
        return total + held2[k - 1]

    def sent(k, carry):
        for j in range(1, subs):
            inner(k, j).wait_send()
        return carry

    lax.fori_loop(1, groups, start, 0)
    start(0, 0)
    lax.fori_loop(1, groups, pass_on, 0)
    total = own_ref[...] + summed(0)
    total = lax.fori_loop(1, groups, take, total)
    lax.fori_loop(0, groups, sent, 0)
    piece_ref[...] = total
    if last:
        full_ref[sub] = total

        def along(j, slot):
            where = (owner, around(sub, j, subs))
            return remote(
                piece_ref, full_ref.at[slot], send4.at[j - 1, 0], recv4.at[j - 1, 0], where
            )

        for j in range(1, subs):
            along(j, sub).start()
        for j in range(1, subs):
            along(j, around(sub, -j, subs)).wait()
    else:
        full_ref[owner * subs + sub] = total
        gather_all(groups, subs, owner, sub, piece_ref, full_ref, send3, recv3, send4, recv4)


def comm_params(collective_id):
    return pltpu.CompilerParams(collective_id=collective_id, has_side_effects=True)


def vmem_specs(count):
    return [pl.BlockSpec(memory_space=pltpu.VMEM)] * count


def semaphores(groups, subs, wide):
    shape = (subs - 1, groups) if wide else (groups - 1,)
    return [pltpu.SemaphoreType.DMA(shape)] * 2


def share(piece, groups, subs):
    return pl.pallas_call(
        functools.partial(share_kernel, groups, subs),
        name="share",
        out_shape=jax.ShapeDtypeStruct((groups * subs,) + piece.shape, jnp.float32),
        in_specs=vmem_specs(1),
        out_specs=vmem_specs(1)[0],
        scratch_shapes=semaphores(groups, subs, False) + semaphores(groups, subs, True),
        compiler_params=comm_params(0),
    )(piece)


def reduce_share(delta, own, groups, subs, last):
    pieces = subs if last else groups * subs
    return pl.pallas_call(
        functools.partial(reduce_share_kernel, groups, subs, last),
        name="reduce_last" if last else "reduce_share",
        out_shape=(
            jax.ShapeDtypeStruct((pieces,) + own.shape, jnp.float32),
            jax.ShapeDtypeStruct(own.shape, jnp.float32),
        ),
        in_specs=vmem_specs(2),
        out_specs=tuple(vmem_specs(2)),
        scratch_shapes=[
            pltpu.VMEM((subs - 1, groups) + own.shape, jnp.float32),
            pltpu.VMEM((groups - 1,) + own.shape, jnp.float32),
            pltpu.VMEM((groups - 1,) + own.shape, jnp.float32),
        ]
        + semaphores(groups, subs, True)
        + semaphores(groups, subs, False) * 2
        + semaphores(groups, subs, True),
        compiler_params=comm_params(2 if last else 1),
    )(delta, own)


def low_high(index, height):
    chunk = lax.shift_right_logical(index, 7)
    if height & (height - 1) == 0:
        chunk = chunk & (height - 1)
    else:
        chunk = lax.rem(chunk, jnp.full_like(chunk, height))
    return index & (LANES - 1), chunk


def gather_rows(table_ref, base, subs, first_row, rows, part, low, chunk):
    out = [jnp.zeros(low.shape, jnp.float32) for _ in range(rows)]
    for sub in range(subs):
        for c in range(part):
            hit = chunk == sub * part + c
            for row in range(rows):
                line = table_ref[base + sub, pl.ds((first_row + row) * part + c, 1), :]
                picked = jnp.take_along_axis(
                    jnp.broadcast_to(line, low.shape), low, axis=1, mode="promise_in_bounds"
                )
                out[row] = jnp.where(hit, picked, out[row])
    return out


def prepare_kernel(groups, subs, part, table_ref, first_ref, second_ref, geo_ref, coef_ref):
    owner = lax.axis_index("owner")

    def body(q, carry):
        low1, chunk1 = low_high(first_ref[q], subs * part)
        low2, chunk2 = low_high(second_ref[q], subs * part)
        normal = [geo_ref[k, q] for k in range(3)]
        cross1 = cross_rows([geo_ref[3 + k, q] for k in range(3)], normal)
        cross2 = cross_rows([geo_ref[6 + k, q] for k in range(3)], normal)
        props1 = gather_rows(table_ref, owner * subs, subs, VEL, PROPS, part, low1, chunk1)
        props2 = gather_rows(table_ref, q * subs, subs, VEL, PROPS, part, low2, chunk2)
        mass = props1[0] + props2[0]
        for k in range(3):
            mass += cross1[k] * cross1[k] * props1[1 + k]
            mass += cross2[k] * cross2[k] * props2[1 + k]
        values = [relax / mass] + props1 + props2
        for k, value in enumerate(values):
            coef_ref[q, k] = value
        return carry

    lax.fori_loop(0, groups, body, 0)


def place(deltas, low, chunk, height):
    rows = len(deltas)
    tall = lax.broadcasted_iota(jnp.int32, (height, LANES), 0)
    wide = lax.broadcasted_iota(jnp.int32, (LANES, LANES), 0)
    left, right = [], []
    coarse = [d.astype(jnp.bfloat16).astype(jnp.float32) for d in deltas]
    fine = [d - c for d, c in zip(deltas, coarse)]
    for i in range(low.shape[0]):
        hit = tall == jnp.broadcast_to(chunk[i : i + 1], (height, LANES))
        block = [
            jnp.where(hit, jnp.broadcast_to(x[i : i + 1], (height, LANES)), 0.0)
            for x in coarse + fine
        ]
        left.append(jnp.concatenate(block, axis=0).astype(jnp.bfloat16))
        right.append(
            jnp.where(wide == jnp.broadcast_to(low[i : i + 1], (LANES, LANES)), 1.0, 0.0).astype(
                jnp.bfloat16
            )
        )
    out = lax.dot_general(
        jnp.concatenate(left, axis=1),
        jnp.concatenate(right, axis=1),
        (((1,), (1,)), ((), ())),
        preferred_element_type=jnp.float32,
    )
    return out[: rows * height] + out[rows * height :]


def iterate_kernel(
    groups, subs, part, table_ref, first_ref, second_ref, geo_ref, coef_ref, target_ref, live_ref,
    impulse_ref, impulse_out, delta_ref, own_acc
):
    owner = lax.axis_index("owner")
    height = subs * part
    own_acc[...] = jnp.zeros_like(own_acc)

    def body(q, carry):
        low1, chunk1 = low_high(first_ref[q], height)
        low2, chunk2 = low_high(second_ref[q], height)
        normal = [geo_ref[k, q] for k in range(3)]
        cross1 = cross_rows([geo_ref[3 + k, q] for k in range(3)], normal)
        cross2 = cross_rows([geo_ref[6 + k, q] for k in range(3)], normal)
        vel1 = gather_rows(table_ref, owner * subs, subs, 0, VEL, part, low1, chunk1)
        vel2 = gather_rows(table_ref, q * subs, subs, 0, VEL, part, low2, chunk2)
        speed = jnp.zeros_like(vel1[0])
        for k in range(3):
            speed += normal[k] * (vel1[k] - vel2[k])
            speed += cross1[k] * vel1[3 + k] - cross2[k] * vel2[3 + k]
        impulse = impulse_ref[q]
        step = (target_ref[q] - speed) * coef_ref[q, 0]
        lane = lax.broadcasted_iota(jnp.int32, impulse.shape, 1)
        fresh = jnp.where(lane < live_ref[q], jnp.maximum(impulse + step, 0.0), impulse)
        impulse_out[q] = fresh
        applied = fresh - impulse
        delta1 = [coef_ref[q, 1] * applied * normal[k] for k in range(3)]
        delta1 += [coef_ref[q, 2 + k] * (applied * cross1[k]) for k in range(3)]
        delta2 = [-(coef_ref[q, 5] * applied * normal[k]) for k in range(3)]
        delta2 += [-(coef_ref[q, 6 + k] * (applied * cross2[k])) for k in range(3)]
        own_acc[...] += place(delta1, low1, chunk1, height)
        there = place(delta2, low2, chunk2, height)
        for sub in range(subs):
            for row in range(VEL):
                start = row * height + sub * part
                delta_ref[q * subs + sub, pl.ds(row * part, part), :] = there[start : start + part]
        return carry

    lax.fori_loop(0, groups, body, 0)
    for sub in range(subs):
        for row in range(VEL):
            start = row * height + sub * part
            delta_ref[owner * subs + sub, pl.ds(row * part, part), :] += own_acc[
                start : start + part, :
            ]


def on_device(
    groups, subs, velocity, properties, first_body, second_body, geometry, target_speed,
    warm_impulse, live_pairs
):
    owned = velocity.shape[1]
    devices = groups * subs
    part = owned // (LANES * subs)
    count = first_body.shape[0]
    rows = count // (groups * LANES)
    block = count // live_pairs.shape[0]
    tiles = (groups, rows, LANES)
    sub = lax.axis_index("sub")

    def own_piece(array):
        cut = lax.dynamic_slice_in_dim(array, sub * (part * LANES), part * LANES, 1)
        return cut.reshape(-1, LANES)

    own = own_piece(velocity)
    table = share(jnp.concatenate([own, own_piece(properties)], axis=0), groups, subs)
    first = first_body.reshape(tiles)
    second = second_body.reshape(tiles)
    geo = geometry.reshape((geometry.shape[0],) + tiles)
    target = target_speed.reshape(tiles)
    impulse = warm_impulse.reshape(tiles)
    slot = jnp.arange(LANES, dtype=jnp.int32)
    rows_per_block = block // LANES
    offset = jnp.arange(count // LANES, dtype=jnp.int32) % rows_per_block * LANES
    bound = jnp.repeat(live_pairs, rows_per_block, total_repeat_length=count // LANES) - offset
    live = jnp.broadcast_to(bound[:, None], (count // LANES, LANES)).reshape(tiles)

    coef = pl.pallas_call(
        functools.partial(prepare_kernel, groups, subs, part),
        name="prepare",
        out_shape=jax.ShapeDtypeStruct((groups, 9, rows, LANES), jnp.float32),
        in_specs=vmem_specs(4),
        out_specs=vmem_specs(1)[0],
    )(table, first, second, geo)

    step = pl.pallas_call(
        functools.partial(iterate_kernel, groups, subs, part),
        name="iterate",
        out_shape=(
            jax.ShapeDtypeStruct(tiles, jnp.float32),
            jax.ShapeDtypeStruct((devices, VEL * part, LANES), jnp.float32),
        ),
        in_specs=vmem_specs(8),
        out_specs=tuple(vmem_specs(2)),
        scratch_shapes=[pltpu.VMEM((VEL * subs * part, LANES), jnp.float32)],
    )
    for iteration in range(ITERS):
        impulse, delta = step(table, first, second, geo, coef, target, live, impulse)
        table, own = reduce_share(delta, own, groups, subs, iteration == ITERS - 1)
    mine = table.reshape(subs, VEL, part, LANES)
    speeds = mine.transpose(1, 0, 2, 3).reshape(VEL, owned)
    return (speeds, impulse.reshape(count))


def solution(mesh):
    groups, subs = mesh.shape["owner"], mesh.shape["sub"]
    return jax.shard_map(
        functools.partial(on_device, groups, subs),
        mesh=mesh,
        in_specs=(
            P(None, "owner"),
            P(None, "owner"),
            P(("owner", "sub")),
            P(("owner", "sub")),
            P(None, ("owner", "sub")),
            P(("owner", "sub")),
            P(("owner", "sub")),
            P(("owner", "sub")),
        ),
        out_specs=(P(None, "owner"), P(("owner", "sub"))),
        check_vma=False,
    )
```

profile of v0, /device:TPU:0, one launch (start us, length us, event | category | flops | bytes accessed | tf_op | source)
XLA Modules:
  0.0 143.5 jit_solution(15179528449244120395)
XLA Ops:
  0.6 0.0 copy-start
  0.7 0.0 copy-start.1
  0.7 0.0 copy-start.2
  0.7 0.7 copy-done.1
  1.3 0.8 gather_fusion
  2.1 0.1 broadcast_in_dim.8
  2.2 0.7 constant_dynamic-slice_fusion
  2.9 0.0 copy-done
  2.9 0.0 copy-start.3
  3.0 0.6 pad_maximum_fusion.piece_ref
  3.6 0.0 copy-done.3
  3.6 0.7 broadcast_in_dim.14.live_ref
  4.3 0.0 copy-done.2
  4.3 0.1 copy.12
  4.4 0.7 slice_bitcast_fusion.geo_ref
  5.1 18.1 %share.1.table_ref = f32[32,40,128]{2,1,0:T(8,128)} custom-call(f32[40,128]{1,0:T(8,128)} %pad_maximum_fusion.piece_ref), custom_call_target="tpu_custom_call" | custom-call | tf_op jit(solution)/shard_map/share/pallas_call | solution.py:189
  23.2 3.7 %prepare.1.coef_ref = f32[8,9,8,128]{3,2,1,0:T(8,128)} custom-call(f32[32,40,128]{2,1,0:T(8,128)} %share.1.table_ref, s32[8,8,128]{2,1,0:T(8,128)} %bitcast.14, s32[8,8,128]{2,1,0:T(8,128)} %bitcast.19, f32[9,8,8,128]{3,2,1,0:T(8,128)} %slice_bitcast_fusion.geo_ref), custom_call_target="tpu_custom_call" | custom-call | tf_op jit(solution)/shard_map/prepare/pallas_call | solution.py:374
  26.9 8.1 %iterate.4 = (f32[8,8,128]{2,1,0:T(8,128)}, f32[32,24,128]{2,1,0:T(8,128)}) custom-call(f32[32,40,128]{2,1,0:T(8,128)} %share.1.table_ref, s32[8,8,128]{2,1,0:T(8,128)} %bitcast.15, s32[8,8,128]{2,1,0:T(8,128)} %bitcast.20, f32[9,8,8,128]{3,2,1,0:T(8,128)} %slice_bitcast_fusion.geo_ref, f32[8,9,8,128]{3,2,1,0:T(8,128)} %prepare.1.coef_ref, ...), custom_call_target="tpu_custom_call" | custom-call | tf_op jit(solution)/shard_map/iterate/pallas_call | solution.py:394
  34.9 23.0 %reduce_share.3 = (f32[32,24,128]{2,1,0:T(8,128)}, f32[24,128]{1,0:T(8,128)}) custom-call(f32[32,24,128]{2,1,0:T(8,128)} %get-tuple-element.29.delta_ref, f32[24,128]{1,0:T(8,128)} %copy-done.3), custom_call_target="tpu_custom_call" | custom-call | tf_op jit(solution)/shard_map/reduce_share/pallas_call | solution.py:202
  57.9 8.0 %iterate.5 = (f32[8,8,128]{2,1,0:T(8,128)}, f32[32,24,128]{2,1,0:T(8,128)}) custom-call(f32[32,24,128]{2,1,0:T(8,128)} %get-tuple-element.30.table_ref, s32[8,8,128]{2,1,0:T(8,128)} %bitcast.16, s32[8,8,128]{2,1,0:T(8,128)} %bitcast.21, f32[9,8,8,128]{3,2,1,0:T(8,128)} %slice_bitcast_fusion.geo_ref, f32[8,9,8,128]{3,2,1,0:T(8,128)} %prepare.1.coef_ref, ...), custom_call_target="tpu_custom_call" | custom-call | tf_op jit(solution)/shard_map/iterate/pallas_call | solution.py:394
  65.9 22.3 %reduce_share.4 = (f32[32,24,128]{2,1,0:T(8,128)}, f32[24,128]{1,0:T(8,128)}) custom-call(f32[32,24,128]{2,1,0:T(8,128)} %get-tuple-element.32.delta_ref, f32[24,128]{1,0:T(8,128)} %get-tuple-element.33.own_ref), custom_call_target="tpu_custom_call" | custom-call | tf_op jit(solution)/shard_map/reduce_share/pallas_call | solution.py:202
  88.2 8.0 %iterate.6 = (f32[8,8,128]{2,1,0:T(8,128)}, f32[32,24,128]{2,1,0:T(8,128)}) custom-call(f32[32,24,128]{2,1,0:T(8,128)} %get-tuple-element.34.table_ref, s32[8,8,128]{2,1,0:T(8,128)} %bitcast.17, s32[8,8,128]{2,1,0:T(8,128)} %bitcast.22, f32[9,8,8,128]{3,2,1,0:T(8,128)} %slice_bitcast_fusion.geo_ref, f32[8,9,8,128]{3,2,1,0:T(8,128)} %prepare.1.coef_ref, ...), custom_call_target="tpu_custom_call" | custom-call | tf_op jit(solution)/shard_map/iterate/pallas_call | solution.py:394
  96.3 22.1 %reduce_share.5 = (f32[32,24,128]{2,1,0:T(8,128)}, f32[24,128]{1,0:T(8,128)}) custom-call(f32[32,24,128]{2,1,0:T(8,128)} %get-tuple-element.36.delta_ref, f32[24,128]{1,0:T(8,128)} %get-tuple-element.37.own_ref), custom_call_target="tpu_custom_call" | custom-call | tf_op jit(solution)/shard_map/reduce_share/pallas_call | solution.py:202
  118.4 8.0 %iterate.7 = (f32[8,8,128]{2,1,0:T(8,128)}, f32[32,24,128]{2,1,0:T(8,128)}) custom-call(f32[32,24,128]{2,1,0:T(8,128)} %get-tuple-element.38.table_ref, s32[8,8,128]{2,1,0:T(8,128)} %bitcast.18, s32[8,8,128]{2,1,0:T(8,128)} %bitcast.23, f32[9,8,8,128]{3,2,1,0:T(8,128)} %slice_bitcast_fusion.geo_ref, f32[8,9,8,128]{3,2,1,0:T(8,128)} %prepare.1.coef_ref, ...), custom_call_target="tpu_custom_call" | custom-call | tf_op jit(solution)/shard_map/iterate/pallas_call | solution.py:394
  126.4 15.7 %reduce_last.1 = (f32[4,24,128]{2,1,0:T(8,128)}, f32[24,128]{1,0:T(8,128)}) custom-call(f32[32,24,128]{2,1,0:T(8,128)} %get-tuple-element.40.delta_ref, f32[24,128]{1,0:T(8,128)} %get-tuple-element.41.own_ref), custom_call_target="tpu_custom_call" | custom-call | tf_op jit(solution)/shard_map/reduce_last/pallas_call | solution.py:202
  142.0 0.8 copy.11
  142.8 0.6 reshape.85
  (5 shorter events, 0.0 us)
Async XLA Ops:
  0.6 2.3 %copy-start = (f32[6,2048]{1,0:T(8,128)S(1)}, f32[6,2048]{1,0:T(8,128)}, u32[]{:S(2)}) copy-start(f32[6,2048]{1,0:T(8,128)} %param.10) | copy-start | bytes 147460
  0.7 0.7 copy-start.1
  0.7 3.6 %copy-start.2 = (f32[9,8192]{1,0:T(8,128)S(1)}, f32[9,8192]{1,0:T(8,128)}, u32[]{:S(2)}) copy-start(f32[9,8192]{1,0:T(8,128)} %param.14) | copy-start | bytes 884740
  2.9 0.6 copy-start.3
where the time goes:
time: 144 us; the launch traced here: 143 us
  Pallas kernels  137 us (95%)
  local copies, waits for them, and re-layouts  5.25 us (4%)
    pallas_call x4, Pallas kernels, reduce_share(): pl.pallas_call(functools.partial(reduce_share_kernel, groups, subs, last)...  83.1 us
    pallas_call x4, Pallas kernels, on_device(): step(table, first, second, geo, coef, target, live, impulse)  32.1 us
    pallas_call x1, Pallas kernels, share(): pl.pallas_call(functools.partial(share_kernel, groups, subs), name='share...  18.1 us
    pallas_call x1, Pallas kernels, on_device(): pl.pallas_call(functools.partial(prepare_kernel, groups, subs, part), nam...  3.66 us

commit v1 on v0

v1 whole, which is shorter than its diff:
```python
import functools

import jax
import jax.numpy as jnp
from jax import lax
from jax.experimental import pallas as pl
from jax.experimental.pallas import tpu as pltpu
from jax.sharding import PartitionSpec as P

ITERS = 4
LANES = 128
SUB = 8
WIDE = 256
VEL = 6
PROPS = 4
MAIL = 8
relax = 0.1
MESH = pl.DeviceIdType.MESH
KEEP_BYTES = 24 * 1024 * 1024


def cross_rows(left, right):
    return [
        left[1] * right[2] - left[2] * right[1],
        left[2] * right[0] - left[0] * right[2],
        left[0] * right[1] - left[1] * right[0],
    ]


def remote(source, target, send_sem, recv_sem, where):
    return pltpu.make_async_remote_copy(
        src_ref=source,
        dst_ref=target,
        send_sem=send_sem,
        recv_sem=recv_sem,
        device_id=where,
        device_id_type=MESH,
    )


def flip(sub, stage):
    step = 2**stage
    return sub + step - 2 * step * ((sub // step) % 2)


def spread(row, height):
    return jnp.broadcast_to(row, (height, LANES))


def kernel(
    groups, subs, height, blocks, keep, relaxed,
    vel_ref, prop_ref, first_ref, second_ref, geo_ref, target_ref, live_ref, imp_ref,
    vel_out, imp_out,
    table, parts, onehot, low_s, chunk_s, jac, gain, tgt, imp, coef, rowbuf, acc,
    mail_out, mail_in, mass_out, mass_in, talk_out, talk_in, red_out, red_in,
    s_mail, r_mail, s_mass, r_mass, s_talk, r_talk, s_red, r_red,
):
    owner, sub = lax.axis_index("owner"), lax.axis_index("sub")
    stages = subs.bit_length() - 1
    rows = VEL * height
    owned = height * WIDE

    def partner(k):
        return lax.rem(owner + k, groups)

    def there(k):
        return lax.rem(groups - k, groups)

    barrier = pltpu.get_barrier_semaphore()

    def signal(k, carry):
        pl.semaphore_signal(
            barrier, inc=1, device_id=(partner(k), sub), device_id_type=MESH
        )
        return carry

    lax.fori_loop(1, groups, signal, 0)
    for stage in range(stages):
        pl.semaphore_signal(
            barrier, inc=1, device_id=(owner, flip(sub, stage)), device_id_type=MESH
        )

    def mail(k):
        return remote(
            mail_out.at[k], mail_in.at[there(k)], s_mail.at[k], r_mail.at[there(k)],
            (partner(k), sub),
        )

    def mail_here(k):
        return remote(
            mail_out.at[k], mail_in.at[k], s_mail.at[k], r_mail.at[k], (partner(k), sub)
        )

    def mass(k):
        return remote(
            mass_out.at[k], mass_in.at[there(k)], s_mass.at[k], r_mass.at[there(k)],
            (partner(k), sub),
        )

    def mass_here(k):
        return remote(
            mass_out.at[k], mass_in.at[k], s_mass.at[k], r_mass.at[k], (partner(k), sub)
        )

    def talk(t, k):
        return remote(
            talk_out.at[t, k], talk_in.at[t, there(k)], s_talk.at[t, k],
            r_talk.at[t, there(k)], (partner(k), sub),
        )

    def talk_here(t, k):
        return remote(
            talk_out.at[t, k], talk_in.at[t, k], s_talk.at[t, k], r_talk.at[t, k],
            (partner(k), sub),
        )

    def part(b):
        return pl.ds(b * SUB, SUB)

    def over_blocks(body):
        if blocks == 1:
            body(0)
        else:
            def run(b, carry):
                body(b)
                return carry

            lax.fori_loop(0, blocks, run, 0)

    def live_of(q, b):
        lane = lax.broadcasted_iota(jnp.int32, (SUB, LANES), 1)
        return lane < live_ref[q, part(b)]

    def local(index):
        return index - lax.div(index, jnp.full_like(index, owned)) * owned

    def write_mail(k):
        q = partner(k)

        def block(b):
            normal = [geo_ref[r, q, part(b)] for r in range(3)]
            cross = cross_rows([geo_ref[6 + r, q, part(b)] for r in range(3)], normal)
            live = live_of(q, b)
            for r, value in enumerate(normal + cross):
                mail_out[k, r, part(b)] = jnp.where(live, -value, 0.0)
            mail_out[k, VEL, part(b)] = local(second_ref[q, part(b)]).astype(jnp.float32)
            mail_out[k, VEL + 1, part(b)] = imp_ref[q, part(b)]

        over_blocks(block)

    def post(k, carry):
        write_mail(k)
        mail(k).start()
        return carry

    pl.semaphore_wait(barrier, groups - 1 + stages)
    lax.fori_loop(1, groups, post, 0)
    write_mail(0)

    for r in range(VEL):
        for c in range(height):
            table[pl.ds(r * height + c, 1), :] = vel_ref[pl.ds(r, 1), pl.ds(c * WIDE, WIDE)]
    for r in range(PROPS):
        for c in range(height):
            rowbuf[pl.ds(r * height + c, 1), :] = prop_ref[pl.ds(r, 1), pl.ds(c * WIDE, WIDE)]
    prop_value = rowbuf[pl.ds(0, PROPS * height), :]
    prop_high = prop_value.astype(jnp.bfloat16)
    prop_rest = prop_value - prop_high.astype(jnp.float32)
    parts[0, pl.ds(0, PROPS * height), :] = prop_high
    parts[1, pl.ds(0, PROPS * height), :] = prop_rest.astype(jnp.bfloat16)

    def hot(low, i):
        tall = lax.broadcasted_iota(jnp.int32, (WIDE, LANES), 0)
        return jnp.where(tall == spread(low[i : i + 1], WIDE), 1.0, 0.0).astype(jnp.bfloat16)

    def hot_tile(side, k, b):
        if keep:
            return onehot[side, k, b]
        low = low_s[side, k, part(b)]
        return jnp.concatenate([hot(low, i) for i in range(SUB)], axis=1)

    def hits(side, k, b):
        tall = lax.broadcasted_iota(jnp.int32, (height, LANES), 0)
        chunk = chunk_s[side, k, part(b)]
        return [tall == spread(chunk[i : i + 1], height) for i in range(SUB)]

    def picked(count, side, k, b):
        tile = hot_tile(side, k, b)
        high = parts[0, pl.ds(0, count * height), :]
        rest = parts[1, pl.ds(0, count * height), :]
        return jnp.dot(high, tile, preferred_element_type=jnp.float32) + jnp.dot(
            rest, tile, preferred_element_type=jnp.float32
        )

    def prepare(side, k, b, index, values):
        low_s[side, k, part(b)] = lax.rem(index, jnp.full_like(index, WIDE))
        chunk_s[side, k, part(b)] = lax.div(index, jnp.full_like(index, WIDE))
        low = low_s[side, k, part(b)]
        if keep:
            for i in range(SUB):
                onehot[side, k, b, :, pl.ds(i * LANES, LANES)] = hot(low, i)
        got = picked(PROPS, side, k, b)
        masks = hits(side, k, b)
        prop = []
        for r in range(PROPS):
            found = []
            for i in range(SUB):
                piece = got[r * height : (r + 1) * height, i * LANES : (i + 1) * LANES]
                found.append(jnp.sum(jnp.where(masks[i], piece, 0.0), axis=0, keepdims=True))
            prop.append(jnp.concatenate(found, axis=0))
        total = prop[0]
        for r in range(VEL):
            jac[side, k, r, part(b)] = values[r]
            gain[side, k, r, part(b)] = prop[max(0, r - 2)] * values[r]
        for r in range(3):
            total += values[3 + r] * values[3 + r] * prop[1 + r]
        mass_out[k, side, part(b)] = total

    def prepare_first(k, carry):
        q = partner(k)

        def block(b):
            normal = [geo_ref[r, q, part(b)] for r in range(3)]
            cross = cross_rows([geo_ref[3 + r, q, part(b)] for r in range(3)], normal)
            prepare(0, k, b, local(first_ref[q, part(b)]), normal + cross)
            tgt[0, k, part(b)] = target_ref[q, part(b)]
            imp[0, k, part(b)] = imp_ref[q, part(b)]

        over_blocks(block)
        return carry

    def prepare_second(source, k):
        def block(b):
            values = [source[k, r, part(b)] for r in range(VEL)]
            prepare(1, k, b, source[k, VEL, part(b)].astype(jnp.int32), values)
            tgt[1, k, part(b)] = jnp.zeros((SUB, LANES), jnp.float32)
            imp[1, k, part(b)] = source[k, VEL + 1, part(b)]

        over_blocks(block)

    lax.fori_loop(0, groups, prepare_first, 0)
    prepare_second(mail_out, 0)

    def receive(k, carry):
        mail_here(k).wait_recv()
        prepare_second(mail_in, k)
        mass(k).start()
        return carry

    lax.fori_loop(1, groups, receive, 0)

    def coefficients(side, k, b, peer):
        value = relaxed / (mass_out[k, side, part(b)] + peer)
        if side == 0:
            value = jnp.where(live_of(partner(k), b), value, 0.0)
        coef[side, k, part(b)] = value

    def settle(k, carry):
        mass_here(k).wait_recv()

        def block(b):
            for side in range(2):
                coefficients(side, k, b, mass_in[k, 1 - side, part(b)])

        over_blocks(block)
        return carry

    def settle_own(b):
        for side in range(2):
            coefficients(side, 0, b, mass_out[0, 1 - side, part(b)])

    def speak(t, k):
        def block(b):
            for side in range(2):
                got = picked(VEL, side, k, b)
                masks = hits(side, k, b)
                found = []
                for i in range(SUB):
                    total = jnp.zeros((height, LANES), jnp.float32)
                    for r in range(VEL):
                        piece = got[r * height : (r + 1) * height, i * LANES : (i + 1) * LANES]
                        line = jac[side, k, r, pl.ds(b * SUB + i, 1)]
                        total += piece * spread(line, height)
                    found.append(
                        jnp.sum(jnp.where(masks[i], total, 0.0), axis=0, keepdims=True)
                    )
                talk_out[t, k, side, part(b)] = tgt[side, k, part(b)] - jnp.concatenate(
                    found, axis=0
                )

        over_blocks(block)

    def place(deltas, side, k, b):
        coarse = [d.astype(jnp.bfloat16).astype(jnp.float32) for d in deltas]
        fine = [d - c for d, c in zip(deltas, coarse)]
        masks = hits(side, k, b)
        left = []
        for i in range(SUB):
            lines = [
                jnp.where(masks[i], spread(x[i : i + 1], height), 0.0) for x in coarse + fine
            ]
            left.append(jnp.concatenate(lines, axis=0).astype(jnp.bfloat16))
        out = lax.dot_general(
            jnp.concatenate(left, axis=1),
            hot_tile(side, k, b),
            (((1,), (1,)), ((), ())),
            preferred_element_type=jnp.float32,
        )
        return out[:rows] + out[rows:]

    def act(t, k, peer_ref):
        def block(b):
            for side in range(2):
                push = talk_out[t, k, side, part(b)] + peer_ref[t, k, 1 - side, part(b)]
                before = imp[side, k, part(b)]
                fresh = jnp.maximum(before + push * coef[side, k, part(b)], 0.0)
                imp[side, k, part(b)] = fresh
                applied = fresh - before
                deltas = [applied * gain[side, k, r, part(b)] for r in range(VEL)]
                acc[...] += place(deltas, side, k, b)

        over_blocks(block)

    def reduce(t, stage):
        return remote(
            red_out.at[t, stage], red_in.at[t, stage], s_red.at[t, stage],
            r_red.at[t, stage], (owner, flip(sub, stage)),
        )

    def iteration(t, carry):
        value = table[...]
        high = value.astype(jnp.bfloat16)
        parts[0] = high
        parts[1] = (value - high.astype(jnp.float32)).astype(jnp.bfloat16)

        def send(k, carry):
            speak(t, k)
            talk(t, k).start()
            return carry

        lax.fori_loop(1, groups, send, 0)
        speak(t, 0)

        @pl.when(t == 0)
        def _():
            over_blocks(settle_own)
            lax.fori_loop(1, groups, settle, 0)

        acc[...] = jnp.zeros_like(acc)
        act(t, 0, talk_out)

        def listen(k, carry):
            talk_here(t, k).wait_recv()
            act(t, k, talk_in)
            return carry

        lax.fori_loop(1, groups, listen, 0)
        total = acc[...]
        for stage in range(stages):
            red_out[t, stage] = total
            reduce(t, stage).start()
            reduce(t, stage).wait_recv()
            total = total + red_in[t, stage]
        table[...] += total
        return carry

    lax.fori_loop(0, ITERS, iteration, 0)

    for r in range(VEL):
        for c in range(height):
            vel_out[pl.ds(r, 1), pl.ds(c * WIDE, WIDE)] = table[pl.ds(r * height + c, 1), :]

    def finish(k, carry):
        imp_out[partner(k)] = imp[0, k]
        return carry

    lax.fori_loop(0, groups, finish, 0)

    def sent(k, carry):
        mail(k).wait_send()
        mass(k).wait_send()
        for t in range(ITERS):
            talk(t, k).wait_send()
        return carry

    lax.fori_loop(1, groups, sent, 0)
    for t in range(ITERS):
        for stage in range(stages):
            reduce(t, stage).wait_send()


def on_device(
    groups, subs, velocity, properties, first_body, second_body, geometry, target_speed,
    warm_impulse, live_pairs
):
    owned = velocity.shape[1]
    height = owned // WIDE
    count = first_body.shape[0]
    rows = count // (groups * LANES)
    blocks = rows // SUB
    tiles = (groups, rows, LANES)
    stages = subs.bit_length() - 1
    keep = 2 * count * WIDE * 2 <= KEEP_BYTES
    kept = (2, groups, blocks, WIDE, SUB * LANES) if keep else (1, 1, 1, 16, LANES)

    rows_per_block = count // live_pairs.shape[0] // LANES
    offset = jnp.arange(count // LANES, dtype=jnp.int32) % rows_per_block * LANES
    bound = jnp.repeat(live_pairs, rows_per_block, total_repeat_length=count // LANES) - offset
    live = jnp.broadcast_to(bound[:, None], (count // LANES, LANES)).reshape(tiles)

    f32 = jnp.float32
    pair = (2, groups, rows, LANES)
    speeds, impulse = pl.pallas_call(
        functools.partial(kernel, groups, subs, height, blocks, keep, relax),
        name="contacts",
        out_shape=(
            jax.ShapeDtypeStruct((VEL, owned), f32),
            jax.ShapeDtypeStruct(tiles, f32),
        ),
        in_specs=[pl.BlockSpec(memory_space=pltpu.VMEM)] * 8,
        out_specs=(pl.BlockSpec(memory_space=pltpu.VMEM),) * 2,
        scratch_shapes=[
            pltpu.VMEM((VEL * height, WIDE), f32),
            pltpu.VMEM((2, VEL * height, WIDE), jnp.bfloat16),
            pltpu.VMEM(kept, jnp.bfloat16),
            pltpu.VMEM(pair, jnp.int32),
            pltpu.VMEM(pair, jnp.int32),
            pltpu.VMEM((2, groups, VEL, rows, LANES), f32),
            pltpu.VMEM((2, groups, VEL, rows, LANES), f32),
            pltpu.VMEM(pair, f32),
            pltpu.VMEM(pair, f32),
            pltpu.VMEM(pair, f32),
            pltpu.VMEM((VEL * height, WIDE), f32),
            pltpu.VMEM((VEL * height, WIDE), f32),
            pltpu.VMEM((groups, MAIL, rows, LANES), f32),
            pltpu.VMEM((groups, MAIL, rows, LANES), f32),
            pltpu.VMEM((groups, 2, rows, LANES), f32),
            pltpu.VMEM((groups, 2, rows, LANES), f32),
            pltpu.VMEM((ITERS, groups, 2, rows, LANES), f32),
            pltpu.VMEM((ITERS, groups, 2, rows, LANES), f32),
            pltpu.VMEM((ITERS, stages, VEL * height, WIDE), f32),
            pltpu.VMEM((ITERS, stages, VEL * height, WIDE), f32),
        ]
        + [pltpu.SemaphoreType.DMA((groups,))] * 4
        + [pltpu.SemaphoreType.DMA((ITERS, groups))] * 2
        + [pltpu.SemaphoreType.DMA((ITERS, stages))] * 2,
        compiler_params=pltpu.CompilerParams(collective_id=0, has_side_effects=True),
    )(
        velocity,
        properties,
        first_body.reshape(tiles),
        second_body.reshape(tiles),
        geometry.reshape((geometry.shape[0],) + tiles),
        target_speed.reshape(tiles),
        live,
        warm_impulse.reshape(tiles),
    )
    return (speeds, impulse.reshape(count))


def solution(mesh):
    groups, subs = mesh.shape["owner"], mesh.shape["sub"]
    return jax.shard_map(
        functools.partial(on_device, groups, subs),
        mesh=mesh,
        in_specs=(
            P(None, "owner"),
            P(None, "owner"),
            P(("owner", "sub")),
            P(("owner", "sub")),
            P(None, ("owner", "sub")),
            P(("owner", "sub")),
            P(("owner", "sub")),
            P(("owner", "sub")),
        ),
        out_specs=(P(None, "owner"), P(("owner", "sub"))),
        check_vma=False,
    )
```

time: 144 us -> 76.2 us (0.53)
  Pallas kernels: 137 us -> 69.8 us
    pallas_call x10 -> x1, Pallas kernels: 137 us -> 69.8 us  [on_device(): pl.pallas_call(functools.partial(kernel, groups, subs, height, blocks, ke...]
    unnamed x9 -> x7, local copies, waits for them, and re-layouts: 0.78 us -> 3.26 us
where the time goes in v1:
time: 76.2 us; the launch traced here: 76 us
  Pallas kernels  69.8 us (92%)
  local copies, waits for them, and re-layouts  5.54 us (7%)
    pallas_call x1, Pallas kernels, on_device(): pl.pallas_call(functools.partial(kernel, groups, subs, height, blocks, ke...  69.8 us
    unnamed x7, local copies, waits for them, and re-layouts  3.26 us

profile of v1, /device:TPU:0, one launch (start us, length us, event | category | flops | bytes accessed | tf_op | source)
XLA Modules:
  0.0 76.0 jit_solution(11681961985277557869)
XLA Ops:
  0.6 0.0 copy-start
  0.6 1.1 %copy.10 = f32[2,8,64,128]{3,2,1,0:T(8,128)S(1)} copy(f32[2,8,64,128]{3,1,2,0:T(8,128)} %bitcast.11) | data formatting | bytes 1048576
  1.8 0.7 slice_bitcast_fusion.geo_ref
  2.5 0.0 copy-done
  2.5 0.8 %gather_fusion = s32[64]{0:T(128)S(1)} fusion(s32[64]{0:T(128)S(1)} %copy-done, s32[1024]{0:T(1024)S(1)} %pad_clamp_fusion), kind=kCustom, calls=%fused_computation | custom fusion | bytes 768 | tf_op jit(solution)/shard_map/jit(_take)/gather | solution.py:408
  3.3 0.1 broadcast_in_dim.8
  3.4 0.7 broadcast_in_dim.14.live_ref
  4.1 69.8 %contacts.1 = (f32[6,2048]{1,0:T(8,128)}, f32[8,8,128]{2,1,0:T(8,128)}) custom-call(f32[6,2048]{1,0:T(8,128)} %vel_ref.1, f32[4,2048]{1,0:T(4,128)} %prop_ref.1, s32[8,8,128]{2,1,0:T(8,128)} %bitcast.12, s32[8,8,128]{2,1,0:T(8,128)} %bitcast.13, f32[9,8,8,128]{3,2,1,0:T(8,128)} %slice_bitcast_fusion.geo_ref, f32[8,8,128]{2,1,0:T(8,128)} %bitcast.14, ...), custom_call_target="tpu_custom_call" | custom-call | tf_op jit(solution)/shard_map/contacts/pallas_call | solution.py:413
  73.9 0.0 copy-start.1
  73.9 1.5 %copy.13 = f32[6,2048]{1,0:T(8,128)} copy(f32[6,2048]{1,0:T(8,128)} %get-tuple-element.20) | data formatting | bytes 98304
  75.4 0.0 copy-done.1
  75.4 0.6 copy.14
  (2 shorter events, 0.0 us)
Async XLA Ops:
  0.6 1.9 %copy-start = (s32[64]{0:T(128)S(1)}, s32[64]{0:T(128)}, u32[]{:S(2)}) copy-start(s32[64]{0:T(128)} %param.17) | copy-start | bytes 772
  73.9 1.5 %copy-start.1 = (f32[8,8,128]{2,1,0:T(8,128)S(1)}, f32[8,8,128]{2,1,0:T(8,128)}, u32[]{:S(2)}) copy-start(f32[8,8,128]{2,1,0:T(8,128)} %get-tuple-element.17) | copy-start | bytes 98308

commit v2 on v1

--- a/solution.py
+++ b/solution.py
@@ -17,6 +17,8 @@
 relax = 0.1
 MESH = pl.DeviceIdType.MESH
 KEEP_BYTES = 24 * 1024 * 1024
+HOT = jnp.float8_e4m3fn
+PAIRED = 2
 
 
 def cross_rows(left, right):
@@ -48,10 +50,10 @@
 
 
 def kernel(
-    groups, subs, height, blocks, keep, relaxed,
-    vel_ref, prop_ref, first_ref, second_ref, geo_ref, target_ref, live_ref, imp_ref,
+    groups, subs, height, blocks, span, keep, relaxed,
+    vel_ref, prop_ref, first_ref, second_ref, raw_ref, target_ref, live_ref, imp_ref,
     vel_out, imp_out,
-    table, parts, onehot, low_s, chunk_s, jac, gain, tgt, imp, coef, rowbuf, acc,
+    geo_ref, table, parts, onehot, low_s, chunk_s, jac, gain, tgt, imp, coef, rowbuf, acc,
     mail_out, mail_in, mass_out, mass_in, talk_out, talk_in, red_out, red_in,
     s_mail, r_mail, s_mass, r_mass, s_talk, r_talk, s_red, r_red,
 ):
@@ -59,6 +61,8 @@
     stages = subs.bit_length() - 1
     rows = VEL * height
     owned = height * WIDE
+    full = (groups - 1) // PAIRED
+    head = groups - PAIRED * full
 
     def partner(k):
         return lax.rem(owner + k, groups)
@@ -129,7 +133,13 @@
 
     def live_of(q, b):
         lane = lax.broadcasted_iota(jnp.int32, (SUB, LANES), 1)
-        return lane < live_ref[q, part(b)]
+        line = lax.broadcasted_iota(jnp.int32, (SUB, LANES), 0)
+        bound = jnp.zeros((SUB, LANES), jnp.int32)
+        for i in range(SUB):
+            row = (q * blocks + b) * SUB + i
+            left = live_ref[row // span] - (row % span) * LANES
+            bound = jnp.where(line == i, left, bound)
+        return lane < bound
 
     def local(index):
         return index - lax.div(index, jnp.full_like(index, owned)) * owned
@@ -138,8 +148,14 @@
         q = partner(k)
 
         def block(b):
-            normal = [geo_ref[r, q, part(b)] for r in range(3)]
-            cross = cross_rows([geo_ref[6 + r, q, part(b)] for r in range(3)], normal)
+            for r in range(9):
+                for i in range(SUB):
+                    start = pl.multiple_of(((q * blocks + b) * SUB + i) * LANES, LANES)
+                    geo_ref[r, k, pl.ds(b * SUB + i, 1), :] = raw_ref[
+                        pl.ds(r, 1), pl.ds(start, LANES)
+                    ]
+            normal = [geo_ref[r, k, part(b)] for r in range(3)]
+            cross = cross_rows([geo_ref[6 + r, k, part(b)] for r in range(3)], normal)
             live = live_of(q, b)
             for r, value in enumerate(normal + cross):
                 mail_out[k, r, part(b)] = jnp.where(live, -value, 0.0)
@@ -148,14 +164,17 @@
 
         over_blocks(block)
 
+    def write(k, carry):
+        write_mail(k)
+        return carry
+
     def post(k, carry):
-        write_mail(k)
         mail(k).start()
         return carry
 
+    lax.fori_loop(0, groups, write, 0)
     pl.semaphore_wait(barrier, groups - 1 + stages)
     lax.fori_loop(1, groups, post, 0)
-    write_mail(0)
 
     for r in range(VEL):
         for c in range(height):
@@ -166,12 +185,12 @@
     prop_value = rowbuf[pl.ds(0, PROPS * height), :]
     prop_high = prop_value.astype(jnp.bfloat16)
     prop_rest = prop_value - prop_high.astype(jnp.float32)
-    parts[0, pl.ds(0, PROPS * height), :] = prop_high
-    parts[1, pl.ds(0, PROPS * height), :] = prop_rest.astype(jnp.bfloat16)
+    parts[pl.ds(0, PROPS * height), :] = prop_high
+    parts[pl.ds(PROPS * height, PROPS * height), :] = prop_rest.astype(jnp.bfloat16)
 
     def hot(low, i):
         tall = lax.broadcasted_iota(jnp.int32, (WIDE, LANES), 0)
-        return jnp.where(tall == spread(low[i : i + 1], WIDE), 1.0, 0.0).astype(jnp.bfloat16)
+        return jnp.where(tall == spread(low[i : i + 1], WIDE), 1.0, 0.0).astype(HOT)
 
     def hot_tile(side, k, b):
         if keep:
@@ -186,11 +205,12 @@
 
     def picked(count, side, k, b):
         tile = hot_tile(side, k, b)
-        high = parts[0, pl.ds(0, count * height), :]
-        rest = parts[1, pl.ds(0, count * height), :]
-        return jnp.dot(high, tile, preferred_element_type=jnp.float32) + jnp.dot(
-            rest, tile, preferred_element_type=jnp.float32
-        )
+        half = count * height
+        both = parts[pl.ds(0, 2 * half), :]
+        out = lax.dot_general(
+            both, tile, (((1,), (0,)), ((), ())), preferred_element_type=jnp.float32
+        )
+        return out[:half] + out[half:]
 
     def prepare(side, k, b, index, values):
         low_s[side, k, part(b)] = lax.rem(index, jnp.full_like(index, WIDE))
@@ -220,8 +240,8 @@
         q = partner(k)
 
         def block(b):
-            normal = [geo_ref[r, q, part(b)] for r in range(3)]
-            cross = cross_rows([geo_ref[3 + r, q, part(b)] for r in range(3)], normal)
+            normal = [geo_ref[r, k, part(b)] for r in range(3)]
+            cross = cross_rows([geo_ref[3 + r, k, part(b)] for r in range(3)], normal)
             prepare(0, k, b, local(first_ref[q, part(b)]), normal + cross)
             tgt[0, k, part(b)] = target_ref[q, part(b)]
             imp[0, k, part(b)] = imp_ref[q, part(b)]
@@ -269,9 +289,9 @@
         for side in range(2):
             coefficients(side, 0, b, mass_out[0, 1 - side, part(b)])
 
-    def speak(t, k):
+    def speak(t, ks):
         def block(b):
-            for side in range(2):
+            for k, side in [(k, side) for k in ks for side in range(2)]:
                 got = picked(VEL, side, k, b)
                 masks = hits(side, k, b)
                 found = []
@@ -308,16 +328,19 @@
         )
         return out[:rows] + out[rows:]
 
-    def act(t, k, peer_ref):
+    def act(t, ks):
         def block(b):
-            for side in range(2):
+            moved = []
+            for k, side in [(k, side) for k in ks for side in range(2)]:
+                peer_ref = talk_out if isinstance(k, int) and k == 0 else talk_in
                 push = talk_out[t, k, side, part(b)] + peer_ref[t, k, 1 - side, part(b)]
                 before = imp[side, k, part(b)]
                 fresh = jnp.maximum(before + push * coef[side, k, part(b)], 0.0)
                 imp[side, k, part(b)] = fresh
                 applied = fresh - before
                 deltas = [applied * gain[side, k, r, part(b)] for r in range(VEL)]
-                acc[...] += place(deltas, side, k, b)
+                moved.append(place(deltas, side, k, b))
+            acc[...] += functools.reduce(jnp.add, moved)
 
         over_blocks(block)
 
@@ -330,16 +353,21 @@
     def iteration(t, carry):
         value = table[...]
         high = value.astype(jnp.bfloat16)
-        parts[0] = high
-        parts[1] = (value - high.astype(jnp.float32)).astype(jnp.bfloat16)
-
-        def send(k, carry):
-            speak(t, k)
-            talk(t, k).start()
+        parts[pl.ds(0, rows), :] = high
+        parts[pl.ds(rows, rows), :] = (value - high.astype(jnp.float32)).astype(jnp.bfloat16)
+
+        def send(ks):
+            speak(t, ks)
+            for k in ks:
+                if not (isinstance(k, int) and k == 0):
+                    talk(t, k).start()
+
+        def send_some(j, carry):
+            send([1 + PAIRED * j + n for n in range(PAIRED)])
             return carry
 
-        lax.fori_loop(1, groups, send, 0)
-        speak(t, 0)
+        lax.fori_loop(0, full, send_some, 0)
+        send(list(range(1 + PAIRED * full, groups)) + [0])
 
         @pl.when(t == 0)
         def _():
@@ -347,14 +375,18 @@
             lax.fori_loop(1, groups, settle, 0)
 
         acc[...] = jnp.zeros_like(acc)
-        act(t, 0, talk_out)
-
-        def listen(k, carry):
-            talk_here(t, k).wait_recv()
-            act(t, k, talk_in)
+        def listen(ks):
+            for k in ks:
+                if not (isinstance(k, int) and k == 0):
+                    talk_here(t, k).wait_recv()
+            act(t, ks)
+
+        def listen_some(j, carry):
+            listen([head + PAIRED * j + n for n in range(PAIRED)])
             return carry
 
-        lax.fori_loop(1, groups, listen, 0)
+        listen(list(range(head)))
+        lax.fori_loop(0, full, listen_some, 0)
         total = acc[...]
         for stage in range(stages):
             red_out[t, stage] = total
@@ -400,29 +432,28 @@
     blocks = rows // SUB
     tiles = (groups, rows, LANES)
     stages = subs.bit_length() - 1
-    keep = 2 * count * WIDE * 2 <= KEEP_BYTES
-    kept = (2, groups, blocks, WIDE, SUB * LANES) if keep else (1, 1, 1, 16, LANES)
+    keep = 2 * count * WIDE <= KEEP_BYTES
+    kept = (2, groups, blocks, WIDE, SUB * LANES) if keep else (1, 1, 1, 32, LANES)
 
     rows_per_block = count // live_pairs.shape[0] // LANES
-    offset = jnp.arange(count // LANES, dtype=jnp.int32) % rows_per_block * LANES
-    bound = jnp.repeat(live_pairs, rows_per_block, total_repeat_length=count // LANES) - offset
-    live = jnp.broadcast_to(bound[:, None], (count // LANES, LANES)).reshape(tiles)
-
     f32 = jnp.float32
     pair = (2, groups, rows, LANES)
     speeds, impulse = pl.pallas_call(
-        functools.partial(kernel, groups, subs, height, blocks, keep, relax),
+        functools.partial(kernel, groups, subs, height, blocks, rows_per_block, keep, relax),
         name="contacts",
         out_shape=(
             jax.ShapeDtypeStruct((VEL, owned), f32),
             jax.ShapeDtypeStruct(tiles, f32),
         ),
-        in_specs=[pl.BlockSpec(memory_space=pltpu.VMEM)] * 8,
+        in_specs=[pl.BlockSpec(memory_space=pltpu.VMEM)] * 6
+        + [pl.BlockSpec(memory_space=pltpu.SMEM)]
+        + [pl.BlockSpec(memory_space=pltpu.VMEM)],
         out_specs=(pl.BlockSpec(memory_space=pltpu.VMEM),) * 2,
         scratch_shapes=[
+            pltpu.VMEM((geometry.shape[0],) + tiles, f32),
             pltpu.VMEM((VEL * height, WIDE), f32),
-            pltpu.VMEM((2, VEL * height, WIDE), jnp.bfloat16),
-            pltpu.VMEM(kept, jnp.bfloat16),
+            pltpu.VMEM((2 * VEL * height, WIDE), jnp.bfloat16),
+            pltpu.VMEM(kept, HOT),
             pltpu.VMEM(pair, jnp.int32),
             pltpu.VMEM(pair, jnp.int32),
             pltpu.VMEM((2, groups, VEL, rows, LANES), f32),
@@ -450,9 +481,9 @@
         properties,
         first_body.reshape(tiles),
         second_body.reshape(tiles),
-        geometry.reshape((geometry.shape[0],) + tiles),
+        geometry,
         target_speed.reshape(tiles),
-        live,
+        live_pairs,
         warm_impulse.reshape(tiles),
     )
     return (speeds, impulse.reshape(count))

time: 76.2 us -> 59.6 us (0.78)
  Pallas kernels: 69.8 us -> 56.7 us
  local copies, waits for them, and re-layouts: 5.54 us -> 2.1 us
    pallas_call x1, Pallas kernels: 69.8 us -> 56.7 us  [on_device(): pl.pallas_call(functools.partial(kernel, groups, subs, height, blocks, ro...]
    unnamed x7 -> x4, local copies, waits for them, and re-layouts: 3.26 us -> 2.1 us
    broadcast_in_dim x2 -> x0, local copies, waits for them, and re-layouts: 0.78 us -> none  [on_device(): jnp.broadcast_to(bound[:, None], (count // LANES, LANES)).reshape(tiles)]
    gather x1 -> x0, local copies, waits for them, and re-layouts: 0.78 us -> none  [on_device(): jnp.repeat(live_pairs, rows_per_block, total_repeat_length=count // LANES)]
where the time goes in v2:
time: 59.6 us; the launch traced here: 59.4 us
  Pallas kernels  56.7 us (95%)
  local copies, waits for them, and re-layouts  2.1 us (4%)
  between operations  0.65 us (1%)
    pallas_call x1, Pallas kernels, on_device(): pl.pallas_call(functools.partial(kernel, groups, subs, height, blocks, ro...  56.7 us
    unnamed x4, local copies, waits for them, and re-layouts  2.1 us

profile of v2, /device:TPU:0, one launch (start us, length us, event | category | flops | bytes accessed | tf_op | source)
XLA Modules:
  0.0 59.4 jit_solution(10296855985983028327)
XLA Ops:
  0.6 56.7 %contacts.1 = (f32[6,2048]{1,0:T(8,128)}, f32[8,8,128]{2,1,0:T(8,128)}) custom-call(f32[6,2048]{1,0:T(8,128)} %vel_ref.1, f32[4,2048]{1,0:T(4,128)} %prop_ref.1, s32[8,8,128]{2,1,0:T(8,128)} %bitcast.5, s32[8,8,128]{2,1,0:T(8,128)} %bitcast.6, f32[9,8192]{1,0:T(8,128)} %raw_ref.1, f32[8,8,128]{2,1,0:T(8,128)} %bitcast.7, s32[64]{0:T(128)} %live_ref.1, ...), custom_call_target="tpu_custom_call" | custom-call | tf_op jit(solution)/shard_map/contacts/pallas_call | solution.py:441
  57.3 0.0 copy-start
  57.3 1.5 %copy.12 = f32[6,2048]{1,0:T(8,128)} copy(f32[6,2048]{1,0:T(8,128)} %get-tuple-element.8) | data formatting | bytes 98304
  58.8 0.0 copy-done
  58.8 0.6 %copy.13 = f32[8192]{0:T(1024)} copy(f32[8192]{0:T(1024)S(1)} %bitcast.9) | data formatting | bytes 65536
Async XLA Ops:
  57.3 1.5 %copy-start = (f32[8,8,128]{2,1,0:T(8,128)S(1)}, f32[8,8,128]{2,1,0:T(8,128)}, u32[]{:S(2)}) copy-start(f32[8,8,128]{2,1,0:T(8,128)} %get-tuple-element.5) | copy-start | bytes 98308

commit v3 on v1

v3 whole, which is shorter than its diff:
```python
import functools

import jax
import jax.numpy as jnp
from jax import lax
from jax.experimental import pallas as pl
from jax.experimental.pallas import tpu as pltpu
from jax.sharding import PartitionSpec as P

ITERS = 4
LANES = 128
SUB = 8
WIDE = 256
VEL = 6
PROPS = 4
MAIL = 7
relax = 0.1
MESH = pl.DeviceIdType.MESH
KEEP_BYTES = 24 * 1024 * 1024
HOT = jnp.float8_e4m3fn
PAIRED = 2


def cross_rows(left, right):
    return [
        left[1] * right[2] - left[2] * right[1],
        left[2] * right[0] - left[0] * right[2],
        left[0] * right[1] - left[1] * right[0],
    ]


def remote(source, target, send_sem, recv_sem, where):
    return pltpu.make_async_remote_copy(
        src_ref=source,
        dst_ref=target,
        send_sem=send_sem,
        recv_sem=recv_sem,
        device_id=where,
        device_id_type=MESH,
    )


def flip(sub, stage):
    step = 2**stage
    return sub + step - 2 * step * ((sub // step) % 2)


def spread(row, height):
    return jnp.broadcast_to(row, (height, LANES))


def kernel(
    groups, subs, height, blocks, span, keep, relaxed,
    vel_any, prop_any, first_any, second_any, raw_any, target_any, live_any, imp_any,
    vel_out, imp_out,
    vel_ref, prop_ref, first_ref, second_ref, raw_ref, target_ref, live_ref, imp_ref,
    geo_ref, table, wide_parts, parts, onehot, low_s, chunk_s, jac, gain, imp, coef, rowbuf,
    acc, mail_out, mail_in, mass_out, mass_in, talk_out, talk_in, red_out, red_in,
    s_load, s_mail, r_mail, s_mass, r_mass, s_talk, r_talk, s_red, r_red,
):
    owner, sub = lax.axis_index("owner"), lax.axis_index("sub")
    stages = subs.bit_length() - 1
    rows = VEL * height
    every = (VEL + PROPS) * height
    owned = height * WIDE
    full = (groups - 1) // PAIRED
    head = groups - PAIRED * full
    mirrored = groups & (groups - 1) == 0

    def partner(k):
        if not mirrored:
            return lax.rem(owner + k, groups)
        q = owner
        for bit in range(groups.bit_length() - 1):
            step = 2**bit
            chosen = lax.rem(lax.div(k, step), 2) if not isinstance(k, int) else k // step % 2
            q = q + chosen * (step - 2 * step * lax.rem(lax.div(owner, step), 2))
        return q

    def there(k):
        return k if mirrored else lax.rem(groups - k, groups)

    barrier = pltpu.get_barrier_semaphore()

    def signal(k, carry):
        pl.semaphore_signal(
            barrier, inc=1, device_id=(partner(k), sub), device_id_type=MESH
        )
        return carry

    lax.fori_loop(1, groups, signal, 0)
    for stage in range(stages):
        pl.semaphore_signal(
            barrier, inc=1, device_id=(owner, flip(sub, stage)), device_id_type=MESH
        )

    loads = [
        pltpu.make_async_copy(source, target, s_load.at[n])
        for n, (source, target) in enumerate(
            [
                (raw_any, raw_ref),
                (live_any, live_ref),
                (second_any, second_ref),
                (first_any, first_ref),
                (vel_any, vel_ref),
                (prop_any, prop_ref),
                (target_any, target_ref),
                (imp_any, imp_ref),
            ]
        )
    ]
    for load in loads:
        load.start()

    def link(source, target, send_sem, recv_sem):
        def outgoing(k, *at):
            return remote(
                source.at[(*at, k)], target.at[(*at, there(k))], send_sem.at[(*at, k)],
                recv_sem.at[(*at, there(k))], (partner(k), sub),
            )

        def incoming(k, *at):
            return remote(
                source.at[(*at, k)], target.at[(*at, k)], send_sem.at[(*at, k)],
                recv_sem.at[(*at, k)], (partner(k), sub),
            )

        return outgoing, incoming

    mail, mail_here = link(mail_out, mail_in, s_mail, r_mail)
    mass, mass_here = link(mass_out, mass_in, s_mass, r_mass)
    talk, talk_here = link(talk_out, talk_in, s_talk, r_talk)

    def part(b):
        return pl.ds(b * SUB, SUB)

    def over_blocks(body):
        if blocks == 1:
            body(0)
        else:
            def run(b, carry):
                body(b)
                return carry

            lax.fori_loop(0, blocks, run, 0)

    def far_first(body):
        def run(j, carry):
            body([groups - 1 - PAIRED * j - n for n in range(PAIRED)])
            return carry

        lax.fori_loop(0, full, run, 0)
        body(list(range(head - 1, -1, -1)))

    def near_first(body):
        def run(j, carry):
            body([head + PAIRED * j + n for n in range(PAIRED)])
            return carry

        body(list(range(head)))
        lax.fori_loop(0, full, run, 0)

    def here(k):
        return isinstance(k, int) and k == 0

    def live_of(q, b):
        lane = lax.broadcasted_iota(jnp.int32, (SUB, LANES), 1)
        line = lax.broadcasted_iota(jnp.int32, (SUB, LANES), 0)
        bound = jnp.zeros((SUB, LANES), jnp.int32)
        for i in range(SUB):
            row = (q * blocks + b) * SUB + i
            left = live_ref[row // span] - (row % span) * LANES
            bound = jnp.where(line == i, left, bound)
        return lane < bound

    def local(index):
        return index - lax.div(index, jnp.full_like(index, owned)) * owned

    def write_mail(k, carry):
        q = partner(k)

        def block(b):
            for r in range(9):
                for i in range(SUB):
                    start = pl.multiple_of(((q * blocks + b) * SUB + i) * LANES, LANES)
                    geo_ref[r, k, pl.ds(b * SUB + i, 1), :] = raw_ref[
                        pl.ds(r, 1), pl.ds(start, LANES)
                    ]
            normal = [geo_ref[r, k, part(b)] for r in range(3)]
            cross = cross_rows([geo_ref[6 + r, k, part(b)] for r in range(3)], normal)
            live = live_of(q, b)
            for r, value in enumerate(normal + cross):
                mail_out[k, r, part(b)] = jnp.where(live, -value, 0.0)
            mail_out[k, VEL, part(b)] = local(second_ref[q, part(b)]).astype(jnp.float32)

        over_blocks(block)
        return carry

    for load in loads[:3]:
        load.wait()
    lax.fori_loop(0, groups, write_mail, 0)
    for load in loads[3:]:
        load.wait()

    for r in range(VEL):
        for c in range(height):
            table[pl.ds(r * height + c, 1), :] = vel_ref[pl.ds(r, 1), pl.ds(c * WIDE, WIDE)]
    for r in range(PROPS):
        for c in range(height):
            rowbuf[pl.ds(r * height + c, 1), :] = prop_ref[pl.ds(r, 1), pl.ds(c * WIDE, WIDE)]
    whole = jnp.concatenate([table[...], rowbuf[...]], axis=0)
    whole_high = whole.astype(jnp.bfloat16)
    wide_parts[pl.ds(0, every), :] = whole_high
    wide_parts[pl.ds(every, every), :] = (whole - whole_high.astype(jnp.float32)).astype(
        jnp.bfloat16
    )

    def hot(low, i):
        tall = lax.broadcasted_iota(jnp.int32, (WIDE, LANES), 0)
        return jnp.where(tall == spread(low[i : i + 1], WIDE), 1.0, 0.0).astype(HOT)

    def hot_tile(side, k, b):
        if keep:
            return onehot[side, k, b]
        low = low_s[side, k, part(b)]
        return jnp.concatenate([hot(low, i) for i in range(SUB)], axis=1)

    def hits(chunk):
        tall = lax.broadcasted_iota(jnp.int32, (height, LANES), 0)
        return [tall == spread(chunk[i : i + 1], height) for i in range(SUB)]

    def picked(values, tile):
        half = values.shape[0] // 2
        out = lax.dot_general(
            values[...], tile, (((1,), (0,)), ((), ())), preferred_element_type=jnp.float32
        )
        return out[:half] + out[half:]

    def lookup(got, masks, lines):
        found = []
        for i in range(SUB):
            total = None
            for r, line in lines:
                piece = got[r * height : (r + 1) * height, i * LANES : (i + 1) * LANES]
                if line is not None:
                    piece = piece * spread(line(i), height)
                total = piece if total is None else total + piece
            found.append(jnp.sum(jnp.where(masks[i], total, 0.0), axis=0, keepdims=True))
        return jnp.concatenate(found, axis=0)

    def prepare(side, k, b, index, values, aim):
        low = lax.rem(index, jnp.full_like(index, WIDE))
        chunk = lax.div(index, jnp.full_like(index, WIDE))
        low_s[side, k, part(b)] = low
        chunk_s[side, k, part(b)] = chunk
        pieces = [hot(low, i) for i in range(SUB)]
        if keep:
            for i in range(SUB):
                onehot[side, k, b, :, pl.ds(i * LANES, LANES)] = pieces[i]
        got = picked(wide_parts, jnp.concatenate(pieces, axis=1))
        masks = hits(chunk)
        prop = [lookup(got, masks, [(VEL + r, None)]) for r in range(PROPS)]
        speed = lookup(
            got, masks, [(r, lambda i, r=r: values[r][i : i + 1]) for r in range(VEL)]
        )
        total = prop[0]
        for r in range(VEL):
            jac[side, k, r, part(b)] = values[r]
            gain[side, k, r, part(b)] = prop[max(0, r - 2)] * values[r]
        for r in range(3):
            total += values[3 + r] * values[3 + r] * prop[1 + r]
        mass_out[k, side, part(b)] = total
        talk_out[0, k, side, part(b)] = aim - speed

    def prepare_first(ks):
        def block(b):
            for k in ks:
                q = partner(k)
                normal = [geo_ref[r, k, part(b)] for r in range(3)]
                cross = cross_rows([geo_ref[3 + r, k, part(b)] for r in range(3)], normal)
                index = local(first_ref[q, part(b)])
                prepare(0, k, b, index, normal + cross, target_ref[q, part(b)])
                start = imp_ref[q, part(b)]
                imp[0, k, part(b)] = start
                mass_out[k, 2, part(b)] = start

        over_blocks(block)

    def prepare_second(ks):
        for k in ks:
            if not here(k):
                mail_here(k).wait_recv()

        def block(b):
            for k in ks:
                source = mail_out if here(k) else mail_in
                values = [source[k, r, part(b)] for r in range(VEL)]
                index = source[k, VEL, part(b)].astype(jnp.int32)
                prepare(1, k, b, index, values, 0.0)

        over_blocks(block)
        for k in ks:
            if not here(k):
                mass(k).start()
                talk(k, 0).start()

    def post(j, carry):
        mail(groups - j).start()
        return carry

    far_first(prepare_first)
    pl.semaphore_wait(barrier, groups - 1 + stages)
    lax.fori_loop(1, groups, post, 0)
    far_first(prepare_second)

    def speak(t):
        def some(ks):
            def block(b):
                for k, side in [(k, side) for k in ks for side in range(2)]:
                    got = picked(parts, hot_tile(side, k, b))
                    masks = hits(chunk_s[side, k, part(b)])
                    lines = [
                        (r, lambda i, r=r: jac[side, k, r, pl.ds(b * SUB + i, 1)])
                        for r in range(VEL)
                    ]
                    aim = target_ref[partner(k), part(b)] if side == 0 else 0.0
                    talk_out[t, k, side, part(b)] = aim - lookup(got, masks, lines)

            over_blocks(block)
            for k in ks:
                if not here(k):
                    talk(k, t).start()

        far_first(some)

    def place(deltas, side, k, b):
        coarse = [d.astype(jnp.bfloat16).astype(jnp.float32) for d in deltas]
        fine = [d - c for d, c in zip(deltas, coarse)]
        masks = hits(chunk_s[side, k, part(b)])
        left = []
        for i in range(SUB):
            lines = [
                jnp.where(masks[i], spread(x[i : i + 1], height), 0.0) for x in coarse + fine
            ]
            left.append(jnp.concatenate(lines, axis=0).astype(jnp.bfloat16))
        out = lax.dot_general(
            jnp.concatenate(left, axis=1),
            hot_tile(side, k, b),
            (((1,), (1,)), ((), ())),
            preferred_element_type=jnp.float32,
        )
        return out[:rows] + out[rows:]

    def settle(k, b):
        peer_ref = mass_out if here(k) else mass_in
        for side in range(2):
            value = relaxed / (mass_out[k, side, part(b)] + peer_ref[k, 1 - side, part(b)])
            if side == 0:
                value = jnp.where(live_of(partner(k), b), value, 0.0)
            coef[side, k, part(b)] = value
        imp[1, k, part(b)] = peer_ref[k, 2, part(b)]

    def act(t, first):
        acc[...] = jnp.zeros_like(acc)

        def some(ks):
            for k in ks:
                if not here(k):
                    talk_here(k, t).wait_recv()
                    if first:
                        mass_here(k).wait_recv()

            def block(b):
                moved = []
                for k in ks:
                    if first:
                        settle(k, b)
                    peer_ref = talk_out if here(k) else talk_in
                    for side in range(2):
                        push = (
                            talk_out[t, k, side, part(b)] + peer_ref[t, k, 1 - side, part(b)]
                        )
                        before = imp[side, k, part(b)]
                        fresh = jnp.maximum(before + push * coef[side, k, part(b)], 0.0)
                        imp[side, k, part(b)] = fresh
                        applied = fresh - before
                        deltas = [applied * gain[side, k, r, part(b)] for r in range(VEL)]
                        moved.append(place(deltas, side, k, b))
                acc[...] += functools.reduce(jnp.add, moved)

            over_blocks(block)

        near_first(some)

    def reduce(t, stage):
        return remote(
            red_out.at[t, stage], red_in.at[t, stage], s_red.at[t, stage],
            r_red.at[t, stage], (owner, flip(sub, stage)),
        )

    def advance(t):
        total = acc[...]
        for stage in range(stages):
            red_out[t, stage] = total
            reduce(t, stage).start()
            reduce(t, stage).wait_recv()
            total = total + red_in[t, stage]
        value = table[...] + total
        table[...] = value
        high = value.astype(jnp.bfloat16)
        parts[pl.ds(0, rows), :] = high
        parts[pl.ds(rows, rows), :] = (value - high.astype(jnp.float32)).astype(jnp.bfloat16)

    act(0, True)
    advance(0)

    def iteration(t, carry):
        speak(t)
        act(t, False)
        advance(t)
        return carry

    lax.fori_loop(1, ITERS, iteration, 0)

    for r in range(VEL):
        for c in range(height):
            vel_out[pl.ds(r, 1), pl.ds(c * WIDE, WIDE)] = table[pl.ds(r * height + c, 1), :]

    def finish(k, carry):
        imp_out[partner(k)] = imp[0, k]
        return carry

    lax.fori_loop(0, groups, finish, 0)

    def sent(k, carry):
        mail(k).wait_send()
        mass(k).wait_send()
        for t in range(ITERS):
            talk(k, t).wait_send()
        return carry

    lax.fori_loop(1, groups, sent, 0)
    for t in range(ITERS):
        for stage in range(stages):
            reduce(t, stage).wait_send()


def on_device(
    groups, subs, velocity, properties, first_body, second_body, geometry, target_speed,
    warm_impulse, live_pairs
):
    owned = velocity.shape[1]
    height = owned // WIDE
    count = first_body.shape[0]
    rows = count // (groups * LANES)
    blocks = rows // SUB
    tiles = (groups, rows, LANES)
    stages = subs.bit_length() - 1
    keep = 2 * count * WIDE <= KEEP_BYTES
    kept = (2, groups, blocks, WIDE, SUB * LANES) if keep else (1, 1, 1, 32, LANES)
    span = count // live_pairs.shape[0] // LANES

    f32 = jnp.float32
    pair = (2, groups, rows, LANES)
    operands = (
        velocity,
        properties,
        first_body.reshape(tiles),
        second_body.reshape(tiles),
        geometry,
        target_speed.reshape(tiles),
        live_pairs,
        warm_impulse.reshape(tiles),
    )
    held = [pltpu.VMEM(x.shape, x.dtype) for x in operands]
    held[6] = pltpu.SMEM(live_pairs.shape, live_pairs.dtype)
    speeds, impulse = pl.pallas_call(
        functools.partial(kernel, groups, subs, height, blocks, span, keep, relax),
        name="contacts",
        out_shape=(
            jax.ShapeDtypeStruct((VEL, owned), f32),
            jax.ShapeDtypeStruct(tiles, f32),
        ),
        in_specs=[pl.BlockSpec(memory_space=pl.ANY)] * 8,
        out_specs=(pl.BlockSpec(memory_space=pltpu.VMEM),) * 2,
        scratch_shapes=held
        + [
            pltpu.VMEM((geometry.shape[0],) + tiles, f32),
            pltpu.VMEM((VEL * height, WIDE), f32),
            pltpu.VMEM((2 * (VEL + PROPS) * height, WIDE), jnp.bfloat16),
            pltpu.VMEM((2 * VEL * height, WIDE), jnp.bfloat16),
            pltpu.VMEM(kept, HOT),
            pltpu.VMEM(pair, jnp.int32),
            pltpu.VMEM(pair, jnp.int32),
            pltpu.VMEM((2, groups, VEL, rows, LANES), f32),
            pltpu.VMEM((2, groups, VEL, rows, LANES), f32),
            pltpu.VMEM(pair, f32),
            pltpu.VMEM(pair, f32),
            pltpu.VMEM((PROPS * height, WIDE), f32),
            pltpu.VMEM((VEL * height, WIDE), f32),
            pltpu.VMEM((groups, MAIL, rows, LANES), f32),
            pltpu.VMEM((groups, MAIL, rows, LANES), f32),
            pltpu.VMEM((groups, 3, rows, LANES), f32),
            pltpu.VMEM((groups, 3, rows, LANES), f32),
            pltpu.VMEM((ITERS, groups, 2, rows, LANES), f32),
            pltpu.VMEM((ITERS, groups, 2, rows, LANES), f32),
            pltpu.VMEM((ITERS, stages, VEL * height, WIDE), f32),
            pltpu.VMEM((ITERS, stages, VEL * height, WIDE), f32),
            pltpu.SemaphoreType.DMA((len(operands),)),
        ]
        + [pltpu.SemaphoreType.DMA((groups,))] * 4
        + [pltpu.SemaphoreType.DMA((ITERS, groups))] * 2
        + [pltpu.SemaphoreType.DMA((ITERS, stages))] * 2,
        compiler_params=pltpu.CompilerParams(collective_id=0, has_side_effects=True),
    )(*operands)
    return (speeds, impulse.reshape(count))


def solution(mesh):
    groups, subs = mesh.shape["owner"], mesh.shape["sub"]
    return jax.shard_map(
        functools.partial(on_device, groups, subs),
        mesh=mesh,
        in_specs=(
            P(None, "owner"),
            P(None, "owner"),
            P(("owner", "sub")),
            P(("owner", "sub")),
            P(None, ("owner", "sub")),
            P(("owner", "sub")),
            P(("owner", "sub")),
            P(("owner", "sub")),
        ),
        out_specs=(P(None, "owner"), P(("owner", "sub"))),
        check_vma=False,
    )
```

time: 76.2 us -> 58.2 us (0.76)
  Pallas kernels: 69.8 us -> 55.3 us
  local copies, waits for them, and re-layouts: 5.54 us -> 2.1 us
    pallas_call x1, Pallas kernels: 69.8 us -> 55.3 us  [on_device(): pl.pallas_call(functools.partial(kernel, groups, subs, height, blocks, sp...]
    unnamed x7 -> x4, local copies, waits for them, and re-layouts: 3.26 us -> 2.1 us
    broadcast_in_dim x2 -> x0, local copies, waits for them, and re-layouts: 0.78 us -> none  [on_device(): jnp.broadcast_to(bound[:, None], (count // LANES, LANES)).reshape(tiles)]
    gather x1 -> x0, local copies, waits for them, and re-layouts: 0.78 us -> none  [on_device(): jnp.repeat(live_pairs, rows_per_block, total_repeat_length=count // LANES)]
where the time goes in v3:
time: 58.2 us; the launch traced here: 58.1 us
  Pallas kernels  55.3 us (95%)
  local copies, waits for them, and re-layouts  2.1 us (4%)
  between operations  0.65 us (1%)
    pallas_call x1, Pallas kernels, on_device(): pl.pallas_call(functools.partial(kernel, groups, subs, height, blocks, sp...  55.3 us
    unnamed x4, local copies, waits for them, and re-layouts  2.1 us

profile of v3, /device:TPU:0, one launch (start us, length us, event | category | flops | bytes accessed | tf_op | source)
XLA Modules:
  0.0 58.1 jit_solution(5744101344497721299)
XLA Ops:
  0.6 55.3 %contacts.1 = (f32[6,2048]{1,0:T(8,128)}, f32[8,8,128]{2,1,0:T(8,128)}) custom-call(f32[6,2048]{1,0:T(8,128)} %vel_any.1, f32[4,2048]{1,0:T(4,128)} %prop_any.1, s32[8,8,128]{2,1,0:T(8,128)} %bitcast.5, s32[8,8,128]{2,1,0:T(8,128)} %bitcast.6, f32[9,8192]{1,0:T(8,128)} %raw_any.1, f32[8,8,128]{2,1,0:T(8,128)} %bitcast.7, s32[64]{0:T(128)} %live_any.1, ...), custom_call_target="tpu_custom_call" | custom-call | tf_op jit(solution)/shard_map/contacts/pallas_call | solution.py:477
  55.9 0.0 copy-start
  56.0 1.5 %copy.12 = f32[6,2048]{1,0:T(8,128)} copy(f32[6,2048]{1,0:T(8,128)} %get-tuple-element.8) | data formatting | bytes 98304
  57.4 0.0 copy-done
  57.4 0.6 %copy.13 = f32[8192]{0:T(1024)} copy(f32[8192]{0:T(1024)S(1)} %bitcast.9) | data formatting | bytes 65536
Async XLA Ops:
  55.9 1.5 %copy-start = (f32[8,8,128]{2,1,0:T(8,128)S(1)}, f32[8,8,128]{2,1,0:T(8,128)}, u32[]{:S(2)}) copy-start(f32[8,8,128]{2,1,0:T(8,128)} %get-tuple-element.5) | copy-start | bytes 98308

commit v4 on v3

--- a/solution.py
+++ b/solution.py
@@ -45,6 +45,13 @@
     return sub + step - 2 * step * ((sub // step) % 2)
 
 
+def across(sub, distance):
+    for stage in range(distance.bit_length()):
+        if distance >> stage & 1:
+            sub = flip(sub, stage)
+    return sub
+
+
 def spread(row, height):
     return jnp.broadcast_to(row, (height, LANES))
 
@@ -59,7 +66,6 @@
     s_load, s_mail, r_mail, s_mass, r_mass, s_talk, r_talk, s_red, r_red,
 ):
     owner, sub = lax.axis_index("owner"), lax.axis_index("sub")
-    stages = subs.bit_length() - 1
     rows = VEL * height
     every = (VEL + PROPS) * height
     owned = height * WIDE
@@ -89,9 +95,9 @@
         return carry
 
     lax.fori_loop(1, groups, signal, 0)
-    for stage in range(stages):
+    for j in range(1, subs):
         pl.semaphore_signal(
-            barrier, inc=1, device_id=(owner, flip(sub, stage)), device_id_type=MESH
+            barrier, inc=1, device_id=(owner, across(sub, j)), device_id_type=MESH
         )
 
     loads = [
@@ -305,13 +311,13 @@
                 talk(k, 0).start()
 
     def post(j, carry):
-        mail(groups - j).start()
+        mail(j).start()
         return carry
 
     far_first(prepare_first)
-    pl.semaphore_wait(barrier, groups - 1 + stages)
+    pl.semaphore_wait(barrier, groups + subs - 2)
     lax.fori_loop(1, groups, post, 0)
-    far_first(prepare_second)
+    near_first(prepare_second)
 
     def speak(t):
         def some(ks):
@@ -392,20 +398,23 @@
 
         near_first(some)
 
-    def reduce(t, stage):
+    def reduce(t, j):
         return remote(
-            red_out.at[t, stage], red_in.at[t, stage], s_red.at[t, stage],
-            r_red.at[t, stage], (owner, flip(sub, stage)),
+            red_out.at[t], red_in.at[t, j], s_red.at[t, j], r_red.at[t, j],
+            (owner, across(sub, j)),
         )
 
     def advance(t):
-        total = acc[...]
-        for stage in range(stages):
-            red_out[t, stage] = total
-            reduce(t, stage).start()
-            reduce(t, stage).wait_recv()
-            total = total + red_in[t, stage]
-        value = table[...] + total
+        red_out[t] = acc[...]
+        for j in range(1, subs):
+            reduce(t, j).start()
+        terms = [acc[...]]
+        for j in range(1, subs):
+            reduce(t, j).wait_recv()
+            terms.append(red_in[t, j])
+        while len(terms) > 1:
+            terms = [a + b for a, b in zip(terms[::2], terms[1::2])]
+        value = table[...] + terms[0]
         table[...] = value
         high = value.astype(jnp.bfloat16)
         parts[pl.ds(0, rows), :] = high
@@ -441,8 +450,8 @@
 
     lax.fori_loop(1, groups, sent, 0)
     for t in range(ITERS):
-        for stage in range(stages):
-            reduce(t, stage).wait_send()
+        for j in range(1, subs):
+            reduce(t, j).wait_send()
 
 
 def on_device(
@@ -455,7 +464,6 @@
     rows = count // (groups * LANES)
     blocks = rows // SUB
     tiles = (groups, rows, LANES)
-    stages = subs.bit_length() - 1
     keep = 2 * count * WIDE <= KEEP_BYTES
     kept = (2, groups, blocks, WIDE, SUB * LANES) if keep else (1, 1, 1, 32, LANES)
     span = count // live_pairs.shape[0] // LANES
@@ -478,8 +486,8 @@
         functools.partial(kernel, groups, subs, height, blocks, span, keep, relax),
         name="contacts",
         out_shape=(
-            jax.ShapeDtypeStruct((VEL, owned), f32),
-            jax.ShapeDtypeStruct(tiles, f32),
+            pltpu.VMEM((VEL, owned), f32),
+            pltpu.VMEM(tiles, f32),
         ),
         in_specs=[pl.BlockSpec(memory_space=pl.ANY)] * 8,
         out_specs=(pl.BlockSpec(memory_space=pltpu.VMEM),) * 2,
@@ -504,13 +512,13 @@
             pltpu.VMEM((groups, 3, rows, LANES), f32),
             pltpu.VMEM((ITERS, groups, 2, rows, LANES), f32),
             pltpu.VMEM((ITERS, groups, 2, rows, LANES), f32),
-            pltpu.VMEM((ITERS, stages, VEL * height, WIDE), f32),
-            pltpu.VMEM((ITERS, stages, VEL * height, WIDE), f32),
+            pltpu.VMEM((ITERS, VEL * height, WIDE), f32),
+            pltpu.VMEM((ITERS, subs, VEL * height, WIDE), f32),
             pltpu.SemaphoreType.DMA((len(operands),)),
         ]
         + [pltpu.SemaphoreType.DMA((groups,))] * 4
         + [pltpu.SemaphoreType.DMA((ITERS, groups))] * 2
-        + [pltpu.SemaphoreType.DMA((ITERS, stages))] * 2,
+        + [pltpu.SemaphoreType.DMA((ITERS, subs))] * 2,
         compiler_params=pltpu.CompilerParams(collective_id=0, has_side_effects=True),
     )(*operands)
     return (speeds, impulse.reshape(count))

time: 58.2 us -> 53.6 us (0.921)
  Pallas kernels: 55.3 us -> 51.5 us
  local copies, waits for them, and re-layouts: 2.1 us -> 1.25 us
    pallas_call x1, Pallas kernels: 55.3 us -> 51.5 us  [on_device(): pl.pallas_call(functools.partial(kernel, groups, subs, height, blocks, sp...]
    unnamed x4 -> x2, local copies, waits for them, and re-layouts: 2.1 us -> 1.25 us
where the time goes in v4:
time: 53.6 us; the launch traced here: 53.4 us
  Pallas kernels  51.5 us (96%)
  local copies, waits for them, and re-layouts  1.25 us (2%)
  between operations  0.64 us (1%)
    pallas_call x1, Pallas kernels, on_device(): pl.pallas_call(functools.partial(kernel, groups, subs, height, blocks, sp...  51.5 us
    unnamed x2, local copies, waits for them, and re-layouts  1.25 us

profile of v4, /device:TPU:0, one launch (start us, length us, event | category | flops | bytes accessed | tf_op | source)
XLA Modules:
  0.0 53.4 jit_solution(14494737580797760001)
XLA Ops:
  0.6 51.5 %contacts.1 = (f32[6,2048]{1,0:T(8,128)S(1)}, f32[8,8,128]{2,1,0:T(8,128)S(1)}) custom-call(f32[6,2048]{1,0:T(8,128)} %vel_any.1, f32[4,2048]{1,0:T(4,128)} %prop_any.1, s32[8,8,128]{2,1,0:T(8,128)} %bitcast.6, s32[8,8,128]{2,1,0:T(8,128)} %bitcast.7, f32[9,8192]{1,0:T(8,128)} %raw_any.1, f32[8,8,128]{2,1,0:T(8,128)} %bitcast.8, s32[64]{0:T(128)} %live_any.1, ...), custom_call_target="tpu_custom_call" | custom-call | tf_op jit(solution)/shard_map/contacts/pallas_call | solution.py:485
  52.2 0.6 %copy.12 = f32[6,2048]{1,0:T(8,128)} copy(f32[6,2048]{1,0:T(8,128)S(1)} %get-tuple-element.6) | data formatting | bytes 98304
  52.8 0.6 %copy.13 = f32[8192]{0:T(1024)} copy(f32[8192]{0:T(1024)S(1)} %bitcast.5) | data formatting | bytes 65536

commit v5 on v4

--- a/solution.py
+++ b/solution.py
@@ -163,7 +163,8 @@
             body([head + PAIRED * j + n for n in range(PAIRED)])
             return carry
 
-        body(list(range(head)))
+        body([0])
+        body(list(range(1, head)))
         lax.fori_loop(0, full, run, 0)
 
     def here(k):
@@ -276,7 +277,7 @@
         for r in range(3):
             total += values[3 + r] * values[3 + r] * prop[1 + r]
         mass_out[k, side, part(b)] = total
-        talk_out[0, k, side, part(b)] = aim - speed
+        mass_out[k, 3 + side, part(b)] = aim - speed
 
     def prepare_first(ks):
         def block(b):
@@ -308,7 +309,6 @@
         for k in ks:
             if not here(k):
                 mass(k).start()
-                talk(k, 0).start()
 
     def post(j, carry):
         mail(j).start()
@@ -372,19 +372,26 @@
         def some(ks):
             for k in ks:
                 if not here(k):
-                    talk_here(k, t).wait_recv()
                     if first:
                         mass_here(k).wait_recv()
+                    else:
+                        talk_here(k, t).wait_recv()
 
             def block(b):
                 moved = []
                 for k in ks:
                     if first:
                         settle(k, b)
-                    peer_ref = talk_out if here(k) else talk_in
+                    if first:
+                        mine_ref, peer_ref = mass_out, mass_out if here(k) else mass_in
+                        at, shift = (k,), 3
+                    else:
+                        mine_ref, peer_ref = talk_out, talk_out if here(k) else talk_in
+                        at, shift = (t, k), 0
                     for side in range(2):
                         push = (
-                            talk_out[t, k, side, part(b)] + peer_ref[t, k, 1 - side, part(b)]
+                            mine_ref[(*at, shift + side, part(b))]
+                            + peer_ref[(*at, shift + 1 - side, part(b))]
                         )
                         before = imp[side, k, part(b)]
                         fresh = jnp.maximum(before + push * coef[side, k, part(b)], 0.0)
@@ -444,7 +451,7 @@
     def sent(k, carry):
         mail(k).wait_send()
         mass(k).wait_send()
-        for t in range(ITERS):
+        for t in range(1, ITERS):
             talk(k, t).wait_send()
         return carry
 
@@ -508,8 +515,8 @@
             pltpu.VMEM((VEL * height, WIDE), f32),
             pltpu.VMEM((groups, MAIL, rows, LANES), f32),
             pltpu.VMEM((groups, MAIL, rows, LANES), f32),
-            pltpu.VMEM((groups, 3, rows, LANES), f32),
-            pltpu.VMEM((groups, 3, rows, LANES), f32),
+            pltpu.VMEM((groups, 5, rows, LANES), f32),
+            pltpu.VMEM((groups, 5, rows, LANES), f32),
             pltpu.VMEM((ITERS, groups, 2, rows, LANES), f32),
             pltpu.VMEM((ITERS, groups, 2, rows, LANES), f32),
             pltpu.VMEM((ITERS, VEL * height, WIDE), f32),

time: 53.6 us -> 53.3 us (level)
  no operation moved by 1% of the time
where the time goes in v5:
time: 53.3 us; the launch traced here: 53.2 us
  Pallas kernels  51.3 us (96%)
  local copies, waits for them, and re-layouts  1.25 us (2%)
  between operations  0.64 us (1%)
    pallas_call x1, Pallas kernels, on_device(): pl.pallas_call(functools.partial(kernel, groups, subs, height, blocks, sp...  51.3 us
    unnamed x2, local copies, waits for them, and re-layouts  1.25 us

profile of v5, /device:TPU:0, one launch (start us, length us, event | category | flops | bytes accessed | tf_op | source)
XLA Modules:
  0.0 53.2 jit_solution(3780231223784189659)
XLA Ops:
  0.6 51.3 %contacts.1 = (f32[6,2048]{1,0:T(8,128)S(1)}, f32[8,8,128]{2,1,0:T(8,128)S(1)}) custom-call(f32[6,2048]{1,0:T(8,128)} %vel_any.1, f32[4,2048]{1,0:T(4,128)} %prop_any.1, s32[8,8,128]{2,1,0:T(8,128)} %bitcast.6, s32[8,8,128]{2,1,0:T(8,128)} %bitcast.7, f32[9,8192]{1,0:T(8,128)} %raw_any.1, f32[8,8,128]{2,1,0:T(8,128)} %bitcast.8, s32[64]{0:T(128)} %live_any.1, ...), custom_call_target="tpu_custom_call" | custom-call | tf_op jit(solution)/shard_map/contacts/pallas_call | solution.py:492
  51.9 0.6 %copy.12 = f32[6,2048]{1,0:T(8,128)} copy(f32[6,2048]{1,0:T(8,128)S(1)} %get-tuple-element.6) | data formatting | bytes 98304
  52.6 0.6 %copy.13 = f32[8192]{0:T(1024)} copy(f32[8192]{0:T(1024)S(1)} %bitcast.5) | data formatting | bytes 65536
